TPU v7x, 32 devices: a whole 2x2x4 slice. The times are simulated.
32 devices in a mesh: context: 2 (over core), tensor: 4 (over y, x), fsdp: 4 (over z).
Axes of the slice: x: 2, y: 2, z: 4, core: 2. Of those that a mesh axis runs over, the one named last changes fastest.
Arguments:
- input_raw: bfloat16 [4, 1024, 5120], P('fsdp', ('context', 'tensor')), may hold values from -6 to 6
- state_proj_raw: bfloat16 [4, 1024, 256], P('fsdp', ('context', 'tensor')), may hold values from -6 to 6
- gate_branch: bfloat16 [4, 1024, 5120], P('fsdp', ('context', 'tensor')), may hold values from -6 to 6
- step_raw: bfloat16 [4, 1024, 80], P('fsdp', ('context', 'tensor')), may hold values from -6 to 6
- convolution_taps: float32 [4, 5376], replicated, may hold values from -3 to 3
- convolution_bias: float32 [5376], replicated, may hold values from -3 to 3
- step_bias: float32 [80], P('tensor'), may hold values from -1.5 to 0.5
- decay_log_rate: float32 [80], P('tensor'), may hold values from -13 to -2, as said below
- skip_weight: float32 [80], P('tensor'), may hold values from 0.5 to 2
- gated_norm_gain: float32 [5120], P('tensor'), may hold values from 0.1 to 1.9
- output_weight: bfloat16 [5120, 2560], P('tensor', 'fsdp'), may hold values from -0.078125 to 0.078125
- adapter_down: bfloat16 [5120, 16], P('tensor'), may hold values from -0.078125 to 0.078125
- adapter_up: bfloat16 [16, 2560], replicated, may hold values from -0.29882812 to 0.29882812
- cotangent: bfloat16 [4, 1024, 2560], P('fsdp', ('context', 'tensor')), may hold values from -6 to 6
Outputs:
- mixed: bfloat16 [4, 1024, 2560], P('fsdp', ('context', 'tensor'))
- grad_a: float32 [5120, 16], P('tensor')
- grad_b: float32 [16, 2560], replicated
Inputs may be any that keep to these rules, and one draw needn't show every extreme that they name: `decay_log_rate`: logarithms of positive decay rates.
All inputs are finite; a program needn't handle non-finite values.
Results may differ from a plain program's by a relative error of at most 0.017.
Values may be sent and summed in bfloat16 or wider, within the bound.
No kernel may reach another device: no remote copies, remote signals or barrier semaphores. Data moves between devices by JAX's collectives and lax.ppermute only.
A program may use at most 128 MiB of HBM per device.

v0:
```python
import math
import jax
import jax.numpy as jnp
from jax import lax
from jax.sharding import PartitionSpec as P

epsilon = 1e-05


def passed_along(value, axis, steps):
    count = lax.axis_size(axis)
    leading, last = (max(0, -steps), min(count, count - steps))
    return lax.ppermute(value, axis, [(source, source + steps) for source in range(leading, last)])


def entering(value, axis, join, neutral):
    count, mine = (lax.axis_size(axis), lax.axis_index(axis))
    pieces = jax.tree.map(lambda part: lax.all_gather(part, axis), value)
    subtotal = jax.tree.map(
        lambda part, zero: jnp.full_like(part, 0) + jnp.asarray(zero, part.dtype), value, neutral
    )

    def lap(position, subtotal):
        longer = join(subtotal, jax.tree.map(lambda part: part[position], pieces))
        return jax.tree.map(lambda new, old: jnp.where(position < mine, new, old), longer, subtotal)

    return lax.fori_loop(0, count - 1, lap, subtotal)


def convolve(values, before, weight, bias_row):
    length = values.shape[0]
    extended = jnp.concatenate([before, values], axis=0)
    pre_act = bias_row[None, :] + weight[0][None, :] * extended[0:length].astype(jnp.float32)
    for tap_index in range(1, weight.shape[0]):
        pre_act = pre_act + weight[tap_index][None, :] * extended[
            tap_index : tap_index + length
        ].astype(jnp.float32)
    return jax.nn.silu(pre_act).astype(jnp.bfloat16)


def ssd_blocks(x_heads, b_rows, c_rows, step_size, log_decay, block_len):
    highest = lax.Precision.HIGHEST
    length = x_heads.shape[0]
    head_count = x_heads.shape[1]
    head_size = x_heads.shape[2]
    state_size = b_rows.shape[1]
    blocks = length // block_len
    causal = jnp.arange(block_len)[:, None] >= jnp.arange(block_len)[None, :]

    def advance(state_now, pieces):
        x_block, b_block, c_block, step_block, decay_block = pieces
        cum_decay = jnp.cumsum(decay_block, axis=0)
        cum_heads = cum_decay.T
        gap_decay = cum_heads[:, :, None] - cum_heads[:, None, :]
        decay_mat = jnp.where(causal[None], jnp.exp(jnp.where(causal[None], gap_decay, 0.0)), 0.0)
        gram_mat = jnp.dot(c_block, b_block.T, precision=highest)
        x_scaled = x_block * step_block[:, :, None]
        y_inner = jnp.einsum(
            "hij,jhp->ihp", decay_mat * gram_mat[None], x_scaled, precision=highest
        )
        y_state = jnp.exp(cum_decay)[:, :, None] * jnp.einsum(
            "in,hpn->ihp", c_block, state_now, precision=highest
        )
        tail_decay = jnp.exp(cum_decay[-1][None, :] - cum_decay)
        state_next = jnp.exp(cum_decay[-1])[:, None, None] * state_now + jnp.einsum(
            "jhp,jn->hpn", x_scaled * tail_decay[:, :, None], b_block, precision=highest
        )
        return (state_next, y_inner + y_state)

    start_state = jnp.zeros((head_count, head_size, state_size), jnp.float32)
    state_end, y_blocks = lax.scan(
        advance,
        start_state,
        (
            x_heads.reshape(blocks, block_len, head_count, head_size),
            b_rows.reshape(blocks, block_len, state_size),
            c_rows.reshape(blocks, block_len, state_size),
            step_size.reshape(blocks, block_len, head_count),
            log_decay.reshape(blocks, block_len, head_count),
        ),
    )
    return (y_blocks.reshape(length, head_count, head_size), state_end)


def chain_states(earlier, later):
    return (earlier[0] + later[0], jnp.exp(later[0])[:, None, None] * earlier[1] + later[1])


def row_slice(values, start_row, row_count):
    return lax.dynamic_slice_in_dim(values, start_row, row_count, 0)


def shards(
    input_raw,
    state_proj_raw,
    gate_branch,
    step_raw,
    convolution_taps,
    convolution_bias,
    step_bias,
    decay_log_rate,
    skip_weight,
    gated_norm_gain,
    output_weight,
    adapter_down,
    adapter_up,
    cotangent,
):
    highest = lax.Precision.HIGHEST
    tok_rows = input_raw.shape[1]
    inner_width = input_raw.shape[2]
    state_size = state_proj_raw.shape[2] // 2
    rim_width = convolution_taps.shape[0] - 1
    joined = jnp.concatenate([input_raw[0], state_proj_raw[0]], axis=1)
    before = passed_along(joined[tok_rows - rim_width :], ("context", "tensor"), 1)
    convolved = convolve(joined, before, convolution_taps, convolution_bias)
    x_heads_raw, z_heads, dt_heads = (
        lax.all_to_all(
            convolved[:, :inner_width], "tensor", split_axis=1, concat_axis=0, tiled=True
        ),
        lax.all_to_all(gate_branch[0], "tensor", split_axis=1, concat_axis=0, tiled=True),
        lax.all_to_all(step_raw[0], "tensor", split_axis=1, concat_axis=0, tiled=True),
    )
    shared = lax.all_gather(convolved[:, inner_width:], "tensor", axis=0, tiled=True)
    span_rows = x_heads_raw.shape[0]
    local_heads = dt_heads.shape[1]
    local_width = x_heads_raw.shape[1]
    head_size = local_width // local_heads
    x_heads = x_heads_raw.astype(jnp.float32).reshape(span_rows, local_heads, head_size)
    b_rows = shared[:, :state_size].astype(jnp.float32)
    c_rows = shared[:, state_size:].astype(jnp.float32)
    step_size = jax.nn.softplus(dt_heads.astype(jnp.float32) + step_bias[None, :])
    log_decay = -step_size * jnp.exp(decay_log_rate)[None, :]
    y_local, state_end = ssd_blocks(
        x_heads, b_rows, c_rows, step_size, log_decay, math.gcd(span_rows, 256)
    )
    log_total = jnp.sum(log_decay, axis=0)
    prior_total, incoming = entering(
        (log_total, state_end),
        "context",
        chain_states,
        (jnp.zeros_like(log_total), jnp.zeros_like(state_end)),
    )
    reach_decay = jnp.exp(jnp.cumsum(log_decay, axis=0))
    y_heads = y_local + reach_decay[:, :, None] * jnp.einsum(
        "tn,hpn->thp", c_rows, incoming, precision=highest
    )
    y_heads = y_heads + skip_weight[None, :, None] * x_heads
    gated = y_heads.reshape(span_rows, local_width) * jax.nn.silu(z_heads.astype(jnp.float32))
    squares = jnp.sum(gated * gated, axis=1)
    gated_output = (gated * gated_norm_gain[None, :]).astype(jnp.bfloat16)
    adapter_piece = jnp.dot(gated_output, adapter_down, preferred_element_type=jnp.float32)
    full_width = local_width * lax.axis_size("tensor")
    columns = lax.all_gather(output_weight, "fsdp", axis=1, tiled=True)
    own_start = lax.axis_index("tensor") * tok_rows
    sum_squares, adapter_all = (
        lax.psum(squares.astype(jnp.bfloat16), "tensor").astype(jnp.float32),
        lax.psum(adapter_piece.astype(jnp.bfloat16), "tensor").astype(jnp.float32),
    )
    scale_all = lax.rsqrt(sum_squares / full_width + epsilon)
    adapter_all = adapter_all.astype(jnp.bfloat16)
    leader = (lax.axis_index("tensor") == 0).astype(jnp.float32)
    start_row = jnp.int32(0)
    frozen_piece = jnp.dot(
        row_slice(gated_output, start_row, lax.axis_size("tensor") * tok_rows),
        columns,
        preferred_element_type=jnp.float32,
    )
    frozen_piece = frozen_piece + 2.0 * leader * jnp.dot(
        row_slice(adapter_all, start_row, lax.axis_size("tensor") * tok_rows),
        adapter_up,
        preferred_element_type=jnp.float32,
    )
    summed = lax.psum_scatter(
        (
            row_slice(scale_all, start_row, lax.axis_size("tensor") * tok_rows)[:, None]
            * frozen_piece
        ).astype(jnp.bfloat16),
        "tensor",
        scatter_dimension=0,
        tiled=True,
    )
    row_norm_scale = row_slice(scale_all, own_start, tok_rows)
    adapter_branch = row_slice(adapter_all, own_start, tok_rows)
    cotangent_rows = cotangent[0]
    token_total = (
        tok_rows * lax.axis_size("context") * lax.axis_size("tensor") * lax.axis_size("fsdp")
    )
    lowrank_factor = 2.0 / math.sqrt(token_total)
    weighted = lowrank_factor * row_norm_scale[:, None] * adapter_branch.astype(jnp.float32)
    grad_b_local = jnp.dot(weighted.T, cotangent_rows.astype(jnp.float32), precision=highest)
    adapter_gradient = (
        lowrank_factor
        * row_norm_scale[:, None]
        * jnp.dot(cotangent_rows, adapter_up.T, preferred_element_type=jnp.float32)
    )
    adapter_span = lax.all_gather(adapter_gradient, "tensor", axis=0, tiled=True)
    grad_a_local = jnp.dot(gated_output.astype(jnp.float32).T, adapter_span, precision=highest)
    grad_a, grad_b_part = lax.psum((grad_a_local, grad_b_local), ("context", "fsdp"))
    grad_b = lax.psum(grad_b_part.astype(jnp.bfloat16), "tensor").astype(jnp.float32)
    return (summed[None], grad_a, grad_b)


def solution(mesh):
    placed = (
        P("fsdp", ("context", "tensor"), None),
        P("fsdp", ("context", "tensor"), None),
        P("fsdp", ("context", "tensor"), None),
        P("fsdp", ("context", "tensor"), None),
        P(),
        P(),
        P("tensor"),
        P("tensor"),
        P("tensor"),
        P("tensor"),
        P("tensor", "fsdp"),
        P("tensor", None),
        P(),
        P("fsdp", ("context", "tensor"), None),
    )
    return jax.shard_map(
        shards,
        mesh=mesh,
        in_specs=placed,
        out_specs=(P("fsdp", ("context", "tensor"), None), P("tensor", None), P()),
        check_vma=False,
    )
```

profile of v0, /device:TPU:0, one launch (start us, length us, event | category | flops | bytes accessed | tf_op | source)
XLA Modules:
  0.0 443.3 jit_solution(7496762377417726398)
XLA Ops:
  8.3 4.9 %collective-permute-start = (bf16[3,5376]{1,0:T(4,128)(2,1)S(1)}, bf16[3,5376]{1,0:T(4,128)(2,1)S(1)}, u32[]{:S(2)}, u32[]{:S(2)}) collective-permute-start(bf16[3,5376]{1,0:T(4,128)(2,1)S(1)} %fusion.75), channel_id=1, source_target_pairs={{0,4},{4,8},{8,12},{12,16},{16,20},{20,24},{24,28},{1,5},{5,9},{9,... | collective-permute-start | bytes 96776 | tf_op jit(solution)/shard_map/ppermute | solution.py:13
  13.2 1.3 all_to_all.30
  14.5 3.3 all-to-all-start
  17.8 1.3 slice_reduce_fusion.6
  19.1 1.7 maximum_maximum_fusion
  20.8 2.1 multiply_convert_fusion.1
  23.1 1.5 copy.81
  24.6 4.2 all-to-all-start.1
  30.3 19.2 %all_gather.21 = bf16[512,256]{1,0:T(8,128)(2,1)S(1)} all-gather(bf16[128,256]{1,0:T(8,128)(2,1)S(1)} %slice.84), channel_id=1, replica_groups=mesh['context'=2,'tensor'=4,'fsdp'=4] {'tensor'}, dimensions={0}, use_global_device_ids=true | all-gather | bytes 327680 | tf_op jit(solution)/shard_map/all_gather | solution.py:124
  51.1 5.4 %copy.68 = f32[4,128,1280]{1,0,2:T(4,128)S(1)} copy(f32[4,128,1280]{1,2,0:T(8,128)S(1)} %convert_bitcast_fusion.1) | data formatting | bytes 5242880 | tf_op jit(solution)/shard_map/convert_element_type | solution.py:129
  56.5 3.4 reshape.159
  59.9 93.5 %while.4 = (s32[]{:T(128)}, f32[20,64,128]{2,1,0:T(8,128)}, f32[2,256,20,64]{1,0,3,2:T(2,128)}, f32[2,256,20]{1,0,2:T(2,128)}, f32[2,256,20,64]{1,0,3,2:T(2,128)...) while((s32[]{:T(128)}, f32[20,64,128]{2,1,0:T(8,128)}, ...), condition=%wide.region_3.4_spmd.clone.clone, body=%wide.region_0.3_spmd.clone.clone.sunk | while | flops 2122191872 | bytes 18280176 | solution.py:71
  63.0 3.1 constant_dynamic-slice_fusion.5
  66.2 6.0 %fusion.115 = f32[256,20,64]{0,2,1:T(8,128)S(1)} fusion(f32[256,256]{1,0:T(8,128)S(1)} %fusion.114, f32[20,256]{1,0:T(8,128)S(1)} %bitcast.176, pred[256,256]{1,0:T(8,128)(4,1)S(1)} %iota_compare_fusion.2, f32[1,256,20,64]{1,0,3,2:T(1,128)S(1)} %constant_dynamic-slice_fusion.5, f32[256,20]{0,1:T(8,128)S(1)} %bitcast.180), kind=kOutput, calls=%fused_computation.15.clone.1 | convolution fusion | flops 1012203520 | bytes 2990080 | tf_op jit(solution)/shard_map/while/body/eval_jaxpr/hij,jhp->ihp/dot_general | solution.py:58
  73.0 2.1 fusion.116
  75.2 1.3 copy.124
  76.5 27.0 %dynamic_update_slice.7 = f32[2,256,20,64]{1,0,3,2:T(2,128)} dynamic-update-slice(f32[2,256,20,64]{1,0,3,2:T(2,128)} %get-tuple-element.267, f32[1,256,20,64]{1,0,3,2:T(1,128)S(1)} %copy.124, s32[]{:T(128)} %get-tuple-element.265, s32[]{:T(128)} %constant.41.clone.1..sunk, s32[]{:T(128)} %constant.41.clone.1..sunk, s32[]{:T(128)} %constant.41.clone.1..sunk) | dynamic-update-slice | bytes 2621444 | tf_op jit(solution)/shard_map/while/body/jit(dynamic_update_index_in_dim)/dynamic_update_slice | solution.py:71
  103.6 2.8 fusion.113
  109.5 3.1 constant_dynamic-slice_fusion.5
  112.7 6.0 %fusion.115 = f32[256,20,64]{0,2,1:T(8,128)S(1)} fusion(f32[256,256]{1,0:T(8,128)S(1)} %fusion.114, f32[20,256]{1,0:T(8,128)S(1)} %bitcast.176, pred[256,256]{1,0:T(8,128)(4,1)S(1)} %iota_compare_fusion.2, f32[1,256,20,64]{1,0,3,2:T(1,128)S(1)} %constant_dynamic-slice_fusion.5, f32[256,20]{0,1:T(8,128)S(1)} %bitcast.180), kind=kOutput, calls=%fused_computation.15.clone.1 | convolution fusion | flops 1012203520 | bytes 2990080 | tf_op jit(solution)/shard_map/while/body/eval_jaxpr/hij,jhp->ihp/dot_general | solution.py:58
  119.5 2.4 fusion.116
  121.9 1.3 copy.124
  123.3 27.0 %dynamic_update_slice.7 = f32[2,256,20,64]{1,0,3,2:T(2,128)} dynamic-update-slice(f32[2,256,20,64]{1,0,3,2:T(2,128)} %get-tuple-element.267, f32[1,256,20,64]{1,0,3,2:T(1,128)S(1)} %copy.124, s32[]{:T(128)} %get-tuple-element.265, s32[]{:T(128)} %constant.41.clone.1..sunk, s32[]{:T(128)} %constant.41.clone.1..sunk, s32[]{:T(128)} %constant.41.clone.1..sunk) | dynamic-update-slice | bytes 2621444 | tf_op jit(solution)/shard_map/while/body/jit(dynamic_update_index_in_dim)/dynamic_update_slice | solution.py:71
  150.3 3.2 fusion.113
  154.8 1.5 copy.77
  156.2 3.5 all-to-all-start.2
  161.3 1.4 reduce-window.16
  164.1 2.4 all-reduce
  166.6 6.9 %all-to-all-done.2 = bf16[128,4,1280]{0,2,1:T(8,128)(2,1)S(1)} async-done(((bf16[128,4,1280]{0,2,1:T(8,128)(2,1)}), bf16[128,4,1280]{0,2,1:T(8,128)(2,1)S(1)}, u32[]{:S(2)}, u32[]{:S(2)}) %all-to-all-start.2) | async-done | bytes 1310752 | tf_op jit(solution)/shard_map/all_to_all | solution.py:121
  174.1 2.0 convert_bitcast_fusion
  176.1 4.3 copy.79
  180.4 4.3 reshape.166
  184.7 2.1 reshape.165
  186.8 4.9 %reshape.152 = f32[512,20,64]{0,2,1:T(8,128)} reshape(f32[2,256,20,64]{1,0,3,2:T(2,128)} %get-tuple-element.72) | data formatting | bytes 5242880 | tf_op jit(solution)/shard_map/reshape | solution.py:82
  191.8 6.3 %multiply_reduce_fusion = (bf16[512]{0:T(512)(128)(2,1)S(1)}, f32[512,20,64]{0,2,1:T(8,128)}) fusion(f32[512,20,64]{0,2,1:T(8,128)S(1)} %copy-done.6, f32[512,20,64]{0,2,1:T(8,128)} %reshape.165, f32[20]{0:T(128)S(1)} %copy-done.22, f32[512,20,64]{0,2,1:T(8,128)} %reshape.152, f32[40,64,128]{2,1,0:T(8,128)} %all-gather.7.cloned.1.call-done, ...), kind=kOutput, calls=%fused_computation.66 | convolution fusion | flops 1014169088 | bytes 11323393 | tf_op jit(solution)/shard_map/tn,hpn->thp/dot_general | solution.py:145
  198.1 3.4 copy.80
  201.5 2.7 fusion.52
  204.7 15.3 %all-reduce.1 = (bf16[512,16]{0,1:T(8,128)(2,1)S(1)}, bf16[512]{0:T(512)(128)(2,1)S(1)}) all-reduce(bf16[512,16]{0,1:T(8,128)(2,1)S(1)} %convolution_convert_fusion, bf16[512]{0:T(512)(128)(2,1)S(1)} %get-tuple-element.195), channel_id=1, replica_groups=mesh['context'=2,'tensor'=4,'fsdp'=4] {'tensor'}, use_global_device_ids=true, to_apply=%region_9.10 | all-reduce | flops 8704 | bytes 34816 | tf_op jit(solution)/shard_map/psum | solution.py:158
  220.6 8.2 %all_gather.27 = f32[512,16]{0,1:T(8,128)S(1)} all-gather(f32[128,16]{0,1:T(8,128)S(1)} %convolution_multiply_fusion.1), channel_id=1, replica_groups=mesh['context'=2,'tensor'=4,'fsdp'=4] {'tensor'}, dimensions={0}, use_global_device_ids=true | all-gather | bytes 40960 | tf_op jit(solution)/shard_map/all_gather | solution.py:197
  228.8 51.7 %all-reduce.9 = bf16[16,2560]{1,0:T(8,128)(2,1)} all-reduce(f32[16,2560]{1,0:T(8,128)S(1)} %fusion.55), channel_id=1, replica_groups=mesh['context'=2,'tensor'=4,'fsdp'=4] {'context','fsdp'}, use_global_device_ids=true, to_apply=%region_12.13 | all-reduce | flops 40960 | bytes 245760 | tf_op jit(solution)/shard_map/psum | solution.py:199
  282.0 9.7 %all-gather.5.cloned.1.call-done = bf16[1280,2560]{1,0:T(8,128)(2,1)} async-done(((bf16[1280,640]{1,0:T(8,128)(2,1)}), bf16[1280,2560]{1,0:T(8,128)(2,1)}) %all-gather.5.cloned.1.call-update) | async-done | bytes 6553616 | tf_op jit(solution)/shard_map/all_gather | solution.py:154
  291.6 5.7 %fusion.84 = f32[512,2560]{1,0:T(8,128)S(1)} fusion(bf16[512,1280]{1,0:T(8,128)(2,1)S(1)} %fusion.52, bf16[1280,2560]{1,0:T(8,128)(2,1)} %all-gather.5.cloned.1.call-done), kind=kOutput, calls=%fused_computation.121 | convolution fusion | flops 3355443200 | bytes 13107200 | tf_op jit(solution)/shard_map/dot_general | solution.py:164
  297.3 2.4 multiply_convert_fusion
  299.8 35.1 %all-reduce.8.cloned.1.call-done = bf16[16,2560]{1,0:T(8,128)(2,1)} async-done(((bf16[16,2560]{1,0:T(8,128)(2,1)}), bf16[16,2560]{1,0:T(8,128)(2,1)}) %all-reduce.8.cloned.1.call-update) | async-done | bytes 81936 | tf_op jit(solution)/shard_map/psum | solution.py:200
  334.9 1.6 convert_element_type.128
  336.4 52.5 %all-reduce.6.cloned.1.call-done = f32[1280,16]{0,1:T(8,128)} async-done(((f32[1280,16]{0,1:T(8,128)}), f32[1280,16]{0,1:T(8,128)}) %all-reduce.6.cloned.1.call-update) | async-done | bytes 81936 | tf_op jit(solution)/shard_map/psum | solution.py:199
  388.9 46.4 %reduce-scatter.2.cloned.1.call-done = bf16[128,2560]{1,0:T(8,128)(2,1)} async-done(((bf16[512,2560]{1,0:T(8,128)(2,1)}), bf16[128,2560]{1,0:T(8,128)(2,1)}) %reduce-scatter.2.cloned.1.call-update) | async-done | bytes 655376 | tf_op jit(solution)/shard_map/reduce_scatter | solution.py:174
  435.3 1.5 copy.140
  (139 shorter events, 19.0 us)
Async XLA Ops:
  7.2 212.8 %copy-start = (bf16[1,128,2560]{2,1,0:T(8,128)(2,1)S(1)}, bf16[1,128,2560]{2,1,0:T(8,128)(2,1)}, u32[]{:S(2)}) copy-start(bf16[1,128,2560]{2,1,0:T(8,128)(2,1)} %param.29) | copy-start | bytes 1966084
  7.2 13.6 %copy-start.5 = (bf16[1,128,5120]{2,1,0:T(8,128)(2,1)S(1)}, bf16[1,128,5120]{2,1,0:T(8,128)(2,1)}, u32[]{:S(2)}) copy-start(bf16[1,128,5120]{2,1,0:T(8,128)(2,1)} %param.16) | copy-start | bytes 3932164
  7.2 13.6 %copy-start.11 = (bf16[1,128,256]{2,1,0:T(8,128)(2,1)S(1)}, bf16[1,128,256]{2,1,0:T(8,128)(2,1)}, u32[]{:S(2)}) copy-start(bf16[1,128,256]{2,1,0:T(8,128)(2,1)} %param.17) | copy-start | bytes 196612
  7.2 13.6 %copy-start.18 = (f32[5376]{0:T(1024)S(1)}, f32[5376]{0:T(1024)}, u32[]{:S(2)}) copy-start(f32[5376]{0:T(1024)} %param.21) | copy-start | bytes 64516
  8.3 10.8 %collective-permute-start = (bf16[3,5376]{1,0:T(4,128)(2,1)S(1)}, bf16[3,5376]{1,0:T(4,128)(2,1)S(1)}, u32[]{:S(2)}, u32[]{:S(2)}) collective-permute-start(bf16[3,5376]{1,0:T(4,128)(2,1)S(1)} %fusion.75), channel_id=1, source_target_pairs={{0,4},{4,8},{8,12},{12,16},{16,20},{20,24},{24,28},{1,5},{5,9},{9,... | collective-permute-start | bytes 96776 | tf_op jit(solution)/shard_map/ppermute | solution.py:13
  14.5 10.1 %all-to-all-start = ((bf16[128,4,20]{0,2,1:T(8,128)(2,1)}), bf16[128,4,20]{0,2,1:T(8,128)(2,1)S(1)}, u32[]{:S(2)}, u32[]{:S(2)}) async-start(bf16[128,4,20]{0,2,1:T(8,128)(2,1)} %all_to_all.30), calls=%async_computation | async-start | bytes 49152 | tf_op jit(solution)/shard_map/all_to_all | solution.py:122
  23.1 5.7 %copy-start.21 = (f32[20]{0:T(128)S(1)}, f32[20]{0:T(128)}, u32[]{:S(2)}) copy-start(f32[20]{0:T(128)} %param.23) | copy-start | bytes 244
  23.1 6.4 %copy-start.20 = (f32[20]{0:T(128)S(1)}, f32[20]{0:T(128)}, u32[]{:S(2)}) copy-start(f32[20]{0:T(128)} %param.22) | copy-start | bytes 244
  24.6 4.2 copy-start.15
  24.6 26.3 %all-to-all-start.1 = ((bf16[128,4,1280]{0,2,1:T(8,128)(2,1)}), bf16[128,4,1280]{0,2,1:T(8,128)(2,1)S(1)}, u32[]{:S(2)}, u32[]{:S(2)}) async-start(bf16[128,4,1280]{0,2,1:T(8,128)(2,1)} %bitcast.3), calls=%async_computation.1 | async-start | bytes 2621440 | tf_op jit(solution)/shard_map/all_to_all | solution.py:118
  28.7 163.0 %all-gather.7.cloned.1.call-start = ((), (), s32[]{:S(2)}) async-start(), calls=%async_computation.8 | async-start | bytes 1966080 | tf_op jit(solution)/shard_map/all_gather | solution.py:18
  28.8 0.6 copy-start.12
  49.5 0.7 copy-start.9
  56.5 3.4 copy-start.1
  63.0 9.1 %copy-start.7 = (f32[1,256,20]{1,2,0:T(8,128)}, f32[1,256,20]{1,2,0:T(8,128)S(1)}, u32[]{:S(2)}) copy-start(f32[1,256,20]{1,2,0:T(8,128)S(1)} %copy.123) | copy-start | bytes 61444 | tf_op jit(solution)/shard_map/while
  109.5 9.1 %copy-start.7 = (f32[1,256,20]{1,2,0:T(8,128)}, f32[1,256,20]{1,2,0:T(8,128)S(1)}, u32[]{:S(2)}) copy-start(f32[1,256,20]{1,2,0:T(8,128)S(1)} %copy.123) | copy-start | bytes 61444 | tf_op jit(solution)/shard_map/while
  153.5 1.3 copy-start.8
  153.5 138.1 %all-gather.5.cloned.1.call-start = ((), (), s32[]{:S(2)}) async-start(), calls=%async_computation.4 | async-start | bytes 8192000 | tf_op jit(solution)/shard_map/all_gather | solution.py:154
  154.8 5.1 %copy-start.23 = (u32[32]{0:T(128)S(1)}, u32[32]{0:T(128)}, u32[]{:S(2)}) copy-start(u32[32]{0:T(128)} %constant.76) | copy-start | bytes 388
  154.8 6.3 %copy-start.13 = (f32[4,128,20]{1,2,0:T(8,128)S(1)}, f32[4,128,20]{1,2,0:T(8,128)}, u32[]{:S(2)}) copy-start(f32[4,128,20]{1,2,0:T(8,128)} %copy-done.12) | copy-start | bytes 122884
  154.8 8.9 %copy-start.16 = (bf16[128,4,20]{0,2,1:T(8,128)(2,1)S(1)}, bf16[128,4,20]{0,2,1:T(8,128)(2,1)}, u32[]{:S(2)}) copy-start(bf16[128,4,20]{0,2,1:T(8,128)(2,1)} %copy-done.15) | copy-start | bytes 61444
  156.2 17.3 %all-to-all-start.2 = ((bf16[128,4,1280]{0,2,1:T(8,128)(2,1)}), bf16[128,4,1280]{0,2,1:T(8,128)(2,1)S(1)}, u32[]{:S(2)}, u32[]{:S(2)}) async-start(bf16[128,4,1280]{0,2,1:T(8,128)(2,1)} %bitcast.12), calls=%async_computation.2 | async-start | bytes 2621440 | tf_op jit(solution)/shard_map/all_to_all | solution.py:121
  159.8 175.1 %all-reduce.8.cloned.1.call-start = ((), (), s32[]{:S(2)}) async-start(), calls=%async_computation.7 | async-start | bytes 163840 | tf_op jit(solution)/shard_map/psum | solution.py:200
  174.1 2.0 copy-start.3
  180.4 4.3 copy-start.2
  186.8 4.9 %copy-start.6 = (f32[512,20,64]{0,2,1:T(8,128)S(1)}, f32[512,20,64]{0,2,1:T(8,128)}, u32[]{:S(2)}) copy-start(f32[512,20,64]{0,2,1:T(8,128)} %reshape.166) | copy-start | bytes 7864324
  186.8 4.9 %copy-start.10 = (bf16[512,256]{1,0:T(8,128)(2,1)S(1)}, bf16[512,256]{1,0:T(8,128)(2,1)}, u32[]{:S(2)}) copy-start(bf16[512,256]{1,0:T(8,128)(2,1)} %copy-done.9) | copy-start | bytes 786436
  186.8 4.9 %copy-start.22 = (f32[20]{0:T(128)S(1)}, f32[20]{0:T(128)}, u32[]{:S(2)}) copy-start(f32[20]{0:T(128)} %param.24) | copy-start | bytes 244
  198.1 3.4 copy-start.4
  198.1 3.4 copy-start.19
  201.5 2.7 copy-start.17
  201.5 18.9 %copy-start.14 = (bf16[16,2560]{1,0:T(8,128)(2,1)S(1)}, bf16[16,2560]{1,0:T(8,128)(2,1)}, u32[]{:S(2)}) copy-start(bf16[16,2560]{1,0:T(8,128)(2,1)} %param.28) | copy-start | bytes 245764
  280.6 108.3 %all-reduce.6.cloned.1.call-start = ((), (), s32[]{:S(2)}) async-start(), calls=%async_computation.6 | async-start | bytes 163840 | tf_op jit(solution)/shard_map/psum | solution.py:199
  281.9 153.3 %reduce-scatter.2.cloned.1.call-start = ((), (), s32[]{:S(2)}) async-start(), calls=%async_computation.5 | async-start | bytes 3276800 | tf_op jit(solution)/shard_map/reduce_scatter | solution.py:174
Sparse Core Ops, SparseCore 0:
  153.6 9.6 all-gather.6
  164.9 126.6 all-gather.4
  295.1 39.6 all-reduce.7
  337.6 51.2 all-reduce.5
  392.3 42.9 reduce-scatter.1
where the time goes:
time: 448 us; the launch traced here: 443 us
  waiting for transfers between devices  151 us (34%)
  local copies, waits for them, and re-layouts  105 us (23%)
  blocking collectives  96.8 us (22%)
  matrix products  41.7 us (9%)
  other arithmetic  17.6 us (4%)
  starting transfers between devices  16 us (4%)
  between operations  14.8 us (3%)
    dynamic_update_slice x4, local copies, waits for them, and re-layouts, ssd_blocks(): lax.scan(advance, start_state, (x_heads.reshape(blocks, block_len, head_c...  56.8 us
    psum x1, waiting for transfers between devices, shards(): lax.psum((grad_a_local, grad_b_local), ('context', 'fsdp'))  52.5 us
    psum x1, blocking collectives, shards(): lax.psum((grad_a_local, grad_b_local), ('context', 'fsdp'))  51.7 us
    reduce_scatter x1, waiting for transfers between devices, shards(): lax.psum_scatter((row_slice(scale_all, start_row, lax.axis_size('tensor')...  46.4 us
    psum x1, waiting for transfers between devices, shards(): lax.psum(grad_b_part.astype(jnp.bfloat16), 'tensor').astype(jnp.float32)  35.1 us
    all_gather x1, blocking collectives, shards(): lax.all_gather(convolved[:, inner_width:], 'tensor', axis=0, tiled=True)  19.2 us
    psum x1, blocking collectives, shards(): lax.psum(adapter_piece.astype(jnp.bfloat16), 'tensor').astype(jnp.float32)  15.3 us
    dot_general x2, matrix products, advance(): jnp.einsum('hij,jhp->ihp', decay_mat * gram_mat[None], x_scaled, precisio...  11.9 us
  transfers between devices with their start and end apart: 9, of which 5 were waited for; matrix products, arithmetic and copies ran while one was open for 13% of the time, Pallas kernels for 0%

commit v1 on v0

--- a/solution.py
+++ b/solution.py
@@ -196,7 +196,7 @@
     )
     adapter_span = lax.all_gather(adapter_gradient, "tensor", axis=0, tiled=True)
     grad_a_local = jnp.dot(gated_output.astype(jnp.float32).T, adapter_span, precision=highest)
-    grad_a, grad_b_part = lax.psum((grad_a_local, grad_b_local), ("context", "fsdp"))
+    grad_a, grad_b_part = lax.psum(lax.psum((grad_a_local, grad_b_local), "fsdp"), "context")
     grad_b = lax.psum(grad_b_part.astype(jnp.bfloat16), "tensor").astype(jnp.float32)
     return (summed[None], grad_a, grad_b)
 

time: 448 us -> 502 us (1.12)
  waiting for transfers between devices: 151 us -> 250 us
  blocking collectives: 96.8 us -> 47.2 us
    all_gather x1, waiting for transfers between devices: 9.67 us -> 116 us  [shards(): columns = lax.all_gather(output_weight, 'fsdp', axis=1, tiled=True)]
    psum x1, blocking collectives: 51.7 us -> 5.15 us  [shards(): lax.psum(lax.psum((grad_a_local, grad_b_local), 'fsdp'), 'context')]
    all_to_all x1, waiting for transfers between devices: 6.92 us -> 0.01 us  [shards(): lax.all_to_all(gate_branch[0], 'tensor', split_axis=1, concat_axis=0, til...]
    psum x1 -> x2, waiting for transfers between devices: 52.5 us -> 54.1 us  [the longest x1 35 us: shards(): lax.psum((grad_a_local, grad_b_local), 'fsdp')]
  transfers between devices with their start and end apart: 9 -> 10, of which waited for: 5 -> 5; matrix products, arithmetic and copies ran while one was open for 13% -> 30% of each run, Pallas kernels for 0% -> 0%
where the time goes in v1:
time: 502 us; the launch traced here: 497 us
  waiting for transfers between devices  250 us (50%)
  local copies, waits for them, and re-layouts  106 us (21%)
  blocking collectives  47.2 us (9%)
  matrix products  42.5 us (8%)
  other arithmetic  18.8 us (4%)
  starting transfers between devices  17 us (3%)
  between operations  15.1 us (3%)
    all_gather x1, waiting for transfers between devices, shards(): columns = lax.all_gather(output_weight, 'fsdp', axis=1, tiled=True)  116 us
    dynamic_update_slice x4, local copies, waits for them, and re-layouts, ssd_blocks(): lax.scan(advance, start_state, (x_heads.reshape(blocks, block_len, head_c...  56.8 us
    reduce_scatter x1, waiting for transfers between devices, shards(): lax.psum_scatter((row_slice(scale_all, start_row, lax.axis_size('tensor')...  44.2 us
    psum x1, waiting for transfers between devices, shards(): lax.psum((grad_a_local, grad_b_local), 'fsdp')  35 us
    psum x1, waiting for transfers between devices, shards(): lax.psum(grad_b_part.astype(jnp.bfloat16), 'tensor').astype(jnp.float32)  34.8 us
    psum x1, waiting for transfers between devices, shards(): lax.psum(lax.psum((grad_a_local, grad_b_local), 'fsdp'), 'context')  19.1 us
    psum x1, blocking collectives, shards(): lax.psum(adapter_piece.astype(jnp.bfloat16), 'tensor').astype(jnp.float32)  16.6 us
    all_gather x1, blocking collectives, shards(): lax.all_gather(convolved[:, inner_width:], 'tensor', axis=0, tiled=True)  15.4 us
  transfers between devices with their start and end apart: 10, of which 5 were waited for; matrix products, arithmetic and copies ran while one was open for 30% of the time, Pallas kernels for 0%

profile of v1, /device:TPU:0, one launch (start us, length us, event | category | flops | bytes accessed | tf_op | source)
XLA Modules:
  0.0 496.9 jit_solution(4775867955171764185)
XLA Ops:
  8.3 4.9 collective-permute-start
  13.2 1.3 all_to_all.30
  14.5 3.3 all-to-all-start
  17.8 1.3 slice_reduce_fusion.6
  19.1 1.7 maximum_maximum_fusion
  20.9 2.1 multiply_convert_fusion.1
  23.1 1.5 copy.81
  24.6 4.3 all-to-all-start.1
  28.9 2.5 copy.77
  34.2 15.4 %all_gather.21 = bf16[512,256]{1,0:T(8,128)(2,1)S(1)} all-gather(bf16[128,256]{1,0:T(8,128)(2,1)S(1)} %slice.84), channel_id=1, replica_groups=mesh['context'=2,'tensor'=4,'fsdp'=4] {'tensor'}, dimensions={0}, use_global_device_ids=true | all-gather | bytes 327680 | tf_op jit(solution)/shard_map/all_gather | solution.py:124
  51.1 4.3 all-to-all-start.2
  55.6 5.4 %copy.68 = f32[4,128,1280]{1,0,2:T(4,128)S(1)} copy(f32[4,128,1280]{1,2,0:T(8,128)S(1)} %convert_bitcast_fusion.1) | data formatting | bytes 5242880 | tf_op jit(solution)/shard_map/convert_element_type | solution.py:129
  61.1 3.4 reshape.159
  64.5 93.6 %while.4 = (s32[]{:T(128)}, f32[20,64,128]{2,1,0:T(8,128)}, f32[2,256,20,64]{1,0,3,2:T(2,128)}, f32[2,256,20]{1,0,2:T(2,128)}, f32[2,256,20,64]{1,0,3,2:T(2,128)...) while((s32[]{:T(128)}, f32[20,64,128]{2,1,0:T(8,128)}, ...), condition=%wide.region_3.4_spmd.clone.clone, body=%wide.region_0.3_spmd.clone.clone.sunk | while | flops 2122191872 | bytes 18280176 | solution.py:71
  67.6 3.1 constant_dynamic-slice_fusion.5
  70.7 6.0 %fusion.115 = f32[256,20,64]{0,2,1:T(8,128)S(1)} fusion(f32[256,256]{1,0:T(8,128)S(1)} %fusion.114, f32[20,256]{1,0:T(8,128)S(1)} %bitcast.176, pred[256,256]{1,0:T(8,128)(4,1)S(1)} %iota_compare_fusion.2, f32[1,256,20,64]{1,0,3,2:T(1,128)S(1)} %constant_dynamic-slice_fusion.5, f32[256,20]{0,1:T(8,128)S(1)} %bitcast.180), kind=kOutput, calls=%fused_computation.15.clone.1 | convolution fusion | flops 1012203520 | bytes 2990080 | tf_op jit(solution)/shard_map/while/body/eval_jaxpr/hij,jhp->ihp/dot_general | solution.py:58
  77.6 2.1 fusion.116
  79.7 1.3 copy.124
  81.1 27.0 %dynamic_update_slice.7 = f32[2,256,20,64]{1,0,3,2:T(2,128)} dynamic-update-slice(f32[2,256,20,64]{1,0,3,2:T(2,128)} %get-tuple-element.269, f32[1,256,20,64]{1,0,3,2:T(1,128)S(1)} %copy.124, s32[]{:T(128)} %get-tuple-element.267, s32[]{:T(128)} %constant.41.clone.1..sunk, s32[]{:T(128)} %constant.41.clone.1..sunk, s32[]{:T(128)} %constant.41.clone.1..sunk) | dynamic-update-slice | bytes 2621444 | tf_op jit(solution)/shard_map/while/body/jit(dynamic_update_index_in_dim)/dynamic_update_slice | solution.py:71
  108.1 2.8 fusion.113
  114.1 3.1 constant_dynamic-slice_fusion.5
  117.2 6.0 %fusion.115 = f32[256,20,64]{0,2,1:T(8,128)S(1)} fusion(f32[256,256]{1,0:T(8,128)S(1)} %fusion.114, f32[20,256]{1,0:T(8,128)S(1)} %bitcast.176, pred[256,256]{1,0:T(8,128)(4,1)S(1)} %iota_compare_fusion.2, f32[1,256,20,64]{1,0,3,2:T(1,128)S(1)} %constant_dynamic-slice_fusion.5, f32[256,20]{0,1:T(8,128)S(1)} %bitcast.180), kind=kOutput, calls=%fused_computation.15.clone.1 | convolution fusion | flops 1012203520 | bytes 2990080 | tf_op jit(solution)/shard_map/while/body/eval_jaxpr/hij,jhp->ihp/dot_general | solution.py:58
  124.1 2.4 fusion.116
  126.5 1.3 copy.124
  127.8 27.0 %dynamic_update_slice.7 = f32[2,256,20,64]{1,0,3,2:T(2,128)} dynamic-update-slice(f32[2,256,20,64]{1,0,3,2:T(2,128)} %get-tuple-element.269, f32[1,256,20,64]{1,0,3,2:T(1,128)S(1)} %copy.124, s32[]{:T(128)} %get-tuple-element.267, s32[]{:T(128)} %constant.41.clone.1..sunk, s32[]{:T(128)} %constant.41.clone.1..sunk, s32[]{:T(128)} %constant.41.clone.1..sunk) | dynamic-update-slice | bytes 2621444 | tf_op jit(solution)/shard_map/while/body/jit(dynamic_update_index_in_dim)/dynamic_update_slice | solution.py:71
  154.9 3.2 fusion.113
  162.4 2.7 all-reduce
  165.1 1.6 copy.78
  166.7 1.9 convert_bitcast_fusion
  168.7 4.1 copy.79
  172.8 4.3 reshape.166
  177.1 2.1 reshape.165
  179.2 4.9 reshape.152
  184.1 6.4 %multiply_reduce_fusion = (bf16[512]{0:T(512)(128)(2,1)S(1)}, f32[512,20,64]{0,2,1:T(8,128)}) fusion(f32[512,20,64]{0,2,1:T(8,128)S(1)} %copy-done.6, f32[512,20,64]{0,2,1:T(8,128)} %reshape.165, f32[20]{0:T(128)S(1)} %copy-done.18, f32[512,20,64]{0,2,1:T(8,128)} %reshape.152, f32[40,64,128]{2,1,0:T(8,128)} %all-gather.7.cloned.1.call-done, ...), kind=kOutput, calls=%fused_computation.66 | convolution fusion | flops 1014169088 | bytes 11323393 | tf_op jit(solution)/shard_map/tn,hpn->thp/dot_general | solution.py:145
  190.5 3.3 copy.80
  193.9 2.7 fusion.52
  197.0 16.6 %all-reduce.2 = (bf16[512,16]{0,1:T(8,128)(2,1)S(1)}, bf16[512]{0:T(512)(128)(2,1)S(1)}) all-reduce(bf16[512,16]{0,1:T(8,128)(2,1)S(1)} %convolution_convert_fusion, bf16[512]{0:T(512)(128)(2,1)S(1)} %get-tuple-element.197), channel_id=1, replica_groups=mesh['context'=2,'tensor'=4,'fsdp'=4] {'tensor'}, use_global_device_ids=true, to_apply=%region_9.10 | all-reduce | flops 8704 | bytes 34816 | tf_op jit(solution)/shard_map/psum | solution.py:158
  215.0 7.3 %all_gather.27 = f32[512,16]{0,1:T(8,128)S(1)} all-gather(f32[128,16]{0,1:T(8,128)S(1)} %convolution_multiply_fusion.1), channel_id=1, replica_groups=mesh['context'=2,'tensor'=4,'fsdp'=4] {'tensor'}, dimensions={0}, use_global_device_ids=true | all-gather | bytes 40960 | tf_op jit(solution)/shard_map/all_gather | solution.py:197
  224.4 35.0 %all-reduce.12.cloned.1.call-done = (f32[1280,16]{0,1:T(8,128)}, f32[16,2560]{1,0:T(8,128)}) async-done(((f32[1280,16]{0,1:T(8,128)}, f32[16,2560]{1,0:T(8,128)}), (f32[1280,16]{0,1:T(8,128)}, f32[16,2560]{1,0:T(8,128)})) %all-reduce.12.cloned.1.call-update) | async-done | bytes 245776 | tf_op jit(solution)/shard_map/psum | solution.py:199
  259.4 5.2 %all-reduce.13 = bf16[16,2560]{1,0:T(8,128)(2,1)} all-reduce(f32[16,2560]{1,0:T(8,128)} %get-tuple-element.186), channel_id=1, replica_groups=mesh['context'=2,'tensor'=4,'fsdp'=4] {'context'}, use_global_device_ids=true, to_apply=%region_14.15 | all-reduce | flops 40960 | bytes 245760 | tf_op jit(solution)/shard_map/psum | solution.py:199
  265.2 115.5 %all-gather.5.cloned.1.call-done = bf16[1280,2560]{1,0:T(8,128)(2,1)} async-done(((bf16[1280,640]{1,0:T(8,128)(2,1)}), bf16[1280,2560]{1,0:T(8,128)(2,1)}) %all-gather.5.cloned.1.call-update) | async-done | bytes 6553616 | tf_op jit(solution)/shard_map/all_gather | solution.py:154
  380.7 5.7 %fusion.84 = f32[512,2560]{1,0:T(8,128)S(1)} fusion(bf16[512,1280]{1,0:T(8,128)(2,1)S(1)} %fusion.52, bf16[1280,2560]{1,0:T(8,128)(2,1)} %all-gather.5.cloned.1.call-done), kind=kOutput, calls=%fused_computation.121 | convolution fusion | flops 3355443200 | bytes 13107200 | tf_op jit(solution)/shard_map/dot_general | solution.py:164
  386.4 2.4 multiply_convert_fusion
  388.9 34.8 %all-reduce.10.cloned.1.call-done = bf16[16,2560]{1,0:T(8,128)(2,1)} async-done(((bf16[16,2560]{1,0:T(8,128)(2,1)}), bf16[16,2560]{1,0:T(8,128)(2,1)}) %all-reduce.10.cloned.1.call-update) | async-done | bytes 81936 | tf_op jit(solution)/shard_map/psum | solution.py:200
  423.6 1.6 convert_element_type.128
  425.2 19.1 %all-reduce.8.cloned.1.call-done = f32[1280,16]{0,1:T(8,128)} async-done(((f32[1280,16]{0,1:T(8,128)}), f32[1280,16]{0,1:T(8,128)}) %all-reduce.8.cloned.1.call-update) | async-done | bytes 81936 | tf_op jit(solution)/shard_map/psum | solution.py:199
  444.3 44.2 %reduce-scatter.2.cloned.1.call-done = bf16[128,2560]{1,0:T(8,128)(2,1)} async-done(((bf16[512,2560]{1,0:T(8,128)(2,1)}), bf16[128,2560]{1,0:T(8,128)(2,1)}) %reduce-scatter.2.cloned.1.call-update) | async-done | bytes 655376 | tf_op jit(solution)/shard_map/reduce_scatter | solution.py:174
  488.5 1.5 copy.142
  (134 shorter events, 21.8 us)
Async XLA Ops:
  7.2 206.5 %copy-start = (bf16[1,128,2560]{2,1,0:T(8,128)(2,1)S(1)}, bf16[1,128,2560]{2,1,0:T(8,128)(2,1)}, u32[]{:S(2)}) copy-start(bf16[1,128,2560]{2,1,0:T(8,128)(2,1)} %param.29) | copy-start | bytes 1966084
  7.2 13.6 %copy-start.5 = (bf16[1,128,5120]{2,1,0:T(8,128)(2,1)S(1)}, bf16[1,128,5120]{2,1,0:T(8,128)(2,1)}, u32[]{:S(2)}) copy-start(bf16[1,128,5120]{2,1,0:T(8,128)(2,1)} %param.16) | copy-start | bytes 3932164
  7.2 13.6 %copy-start.10 = (bf16[1,128,256]{2,1,0:T(8,128)(2,1)S(1)}, bf16[1,128,256]{2,1,0:T(8,128)(2,1)}, u32[]{:S(2)}) copy-start(bf16[1,128,256]{2,1,0:T(8,128)(2,1)} %param.17) | copy-start | bytes 196612
  7.2 13.6 %copy-start.14 = (f32[5376]{0:T(1024)S(1)}, f32[5376]{0:T(1024)}, u32[]{:S(2)}) copy-start(f32[5376]{0:T(1024)} %param.21) | copy-start | bytes 64516
  8.3 10.8 %collective-permute-start = (bf16[3,5376]{1,0:T(4,128)(2,1)S(1)}, bf16[3,5376]{1,0:T(4,128)(2,1)S(1)}, u32[]{:S(2)}, u32[]{:S(2)}) collective-permute-start(bf16[3,5376]{1,0:T(4,128)(2,1)S(1)} %fusion.75), channel_id=1, source_target_pairs={{0,4},{4,8},{8,12},{12,16},{16,20},{20,24},{24,28},{1,5},{5,9},{9,... | collective-permute-start | bytes 96776 | tf_op jit(solution)/shard_map/ppermute | solution.py:13
  14.5 10.1 %all-to-all-start = ((bf16[128,4,20]{0,2,1:T(8,128)(2,1)}), bf16[128,4,20]{0,2,1:T(8,128)(2,1)S(1)}, u32[]{:S(2)}, u32[]{:S(2)}) async-start(bf16[128,4,20]{0,2,1:T(8,128)(2,1)} %all_to_all.30), calls=%async_computation | async-start | bytes 49152 | tf_op jit(solution)/shard_map/all_to_all | solution.py:122
  23.1 5.8 %copy-start.17 = (f32[20]{0:T(128)S(1)}, f32[20]{0:T(128)}, u32[]{:S(2)}) copy-start(f32[20]{0:T(128)} %param.23) | copy-start | bytes 244
  24.6 8.1 %copy-start.12 = (bf16[128,4,20]{0,2,1:T(8,128)(2,1)}, bf16[128,4,20]{0,2,1:T(8,128)(2,1)S(1)}, u32[]{:S(2)}) copy-start(bf16[128,4,20]{0,2,1:T(8,128)(2,1)S(1)} %all-to-all-done) | copy-start | bytes 61444
  24.6 6.8 %copy-start.19 = (u32[32]{0:T(128)S(1)}, u32[32]{0:T(128)}, u32[]{:S(2)}) copy-start(u32[32]{0:T(128)} %constant.76) | copy-start | bytes 388
  24.6 8.8 %copy-start.16 = (f32[20]{0:T(128)S(1)}, f32[20]{0:T(128)}, u32[]{:S(2)}) copy-start(f32[20]{0:T(128)} %param.22) | copy-start | bytes 244
  24.6 26.5 %all-to-all-start.1 = ((bf16[128,4,1280]{0,2,1:T(8,128)(2,1)}), bf16[128,4,1280]{0,2,1:T(8,128)(2,1)S(1)}, u32[]{:S(2)}, u32[]{:S(2)}) async-start(bf16[128,4,1280]{0,2,1:T(8,128)(2,1)} %bitcast.3), calls=%async_computation.1 | async-start | bytes 2621440 | tf_op jit(solution)/shard_map/all_to_all | solution.py:118
  49.6 0.7 copy-start.8
  51.1 114.0 %all-to-all-start.2 = ((bf16[128,4,1280]{0,2,1:T(8,128)(2,1)}), bf16[128,4,1280]{0,2,1:T(8,128)(2,1)}, u32[]{:S(2)}, u32[]{:S(2)}) async-start(bf16[128,4,1280]{0,2,1:T(8,128)(2,1)} %bitcast.12), calls=%async_computation.2 | async-start | bytes 2621440 | tf_op jit(solution)/shard_map/all_to_all | solution.py:121
  55.4 128.7 %all-gather.7.cloned.1.call-start = ((), (), s32[]{:S(2)}) async-start(), calls=%async_computation.8 | async-start | bytes 1966080 | tf_op jit(solution)/shard_map/all_gather | solution.py:18
  61.1 3.4 copy-start.1
  67.6 9.1 %copy-start.7 = (f32[1,256,20]{1,2,0:T(8,128)}, f32[1,256,20]{1,2,0:T(8,128)S(1)}, u32[]{:S(2)}) copy-start(f32[1,256,20]{1,2,0:T(8,128)S(1)} %copy.123) | copy-start | bytes 61444 | tf_op jit(solution)/shard_map/while
  114.0 9.1 %copy-start.7 = (f32[1,256,20]{1,2,0:T(8,128)}, f32[1,256,20]{1,2,0:T(8,128)S(1)}, u32[]{:S(2)}) copy-start(f32[1,256,20]{1,2,0:T(8,128)S(1)} %copy.123) | copy-start | bytes 61444 | tf_op jit(solution)/shard_map/while
  158.1 101.4 %all-reduce.12.cloned.1.call-start = ((), (), s32[]{:S(2)}) async-start(), calls=%async_computation.9 | async-start | bytes 491520 | tf_op jit(solution)/shard_map/psum | solution.py:199
  166.7 2.0 copy-start.3
  172.8 4.3 copy-start.2
  179.2 4.9 copy-start.6
  179.2 4.9 copy-start.9
  179.2 4.9 copy-start.18
  190.5 3.3 copy-start.4
  190.5 3.3 copy-start.15
  193.8 2.7 copy-start.13
  193.8 20.9 %copy-start.11 = (bf16[16,2560]{1,0:T(8,128)(2,1)S(1)}, bf16[16,2560]{1,0:T(8,128)(2,1)}, u32[]{:S(2)}) copy-start(bf16[16,2560]{1,0:T(8,128)(2,1)} %param.28) | copy-start | bytes 245764
  223.6 157.1 %all-gather.5.cloned.1.call-start = ((), (), s32[]{:S(2)}) async-start(), calls=%async_computation.4 | async-start | bytes 8192000 | tf_op jit(solution)/shard_map/all_gather | solution.py:154
  224.3 199.3 %all-reduce.10.cloned.1.call-start = ((), (), s32[]{:S(2)}) async-start(), calls=%async_computation.7 | async-start | bytes 163840 | tf_op jit(solution)/shard_map/psum | solution.py:200
  264.6 179.7 %all-reduce.8.cloned.1.call-start = ((), (), s32[]{:S(2)}) async-start(), calls=%async_computation.6 | async-start | bytes 163840 | tf_op jit(solution)/shard_map/psum | solution.py:199
  265.2 223.3 %reduce-scatter.2.cloned.1.call-start = ((), (), s32[]{:S(2)}) async-start(), calls=%async_computation.5 | async-start | bytes 3276800 | tf_op jit(solution)/shard_map/reduce_scatter | solution.py:174
Sparse Core Ops, SparseCore 0:
  158.2 11.0 all-gather.6
  223.7 35.6 all-reduce.11
  261.0 119.6 all-gather.4
  384.1 39.5 all-reduce.9
  425.8 18.4 all-reduce.7
  447.7 40.7 reduce-scatter.1
